TPU v7x, 32 devices: a whole 2x2x4 slice. The times are simulated.
32 devices in a mesh: rep: 4 (over y, x), feat: 8 (over z, core).
Axes of the slice: x: 2, y: 2, z: 4, core: 2. Of those that a mesh axis runs over, the one named last changes fastest.
Arguments:
- basis: float32 [4, 64, 32768], P('rep', None, 'feat'), may hold values from -6 to 6
- stream: bfloat16 [4, 2, 128, 32768], P('rep', None, None, 'feat'), may hold values from -6 to 6
Outputs:
- new_basis: float32 [4, 64, 32768], P('rep', None, 'feat')
All inputs are finite; a program needn't handle non-finite values.
Results may differ from a plain program's by a relative error of at most 0.0003.
Values sent between devices are 32-bit elements; how exact they have to be, the bound alone decides.
A program may use at most 64 MiB of HBM per device.

v0:
```python
import functools

import jax
import jax.numpy as jnp
from jax import lax
from jax.experimental import pallas as pl
from jax.experimental.pallas import tpu as pltpu
from jax.sharding import PartitionSpec as P

learn_rate = 0.5
LANE = 128
PLAN = (2, 18, 3, 1)
MESH = pl.DeviceIdType.MESH
NN = (((1,), (0,)), ((), ()))
NT = (((1,), (1,)), ((), ()))


def exact_dot(left, right, dims):
    return lax.dot_general(
        left, right, dims, precision=lax.Precision.HIGHEST, preferred_element_type=jnp.float32
    )


def fast_dot(left, right, dims):
    return lax.dot_general(left, right, dims, preferred_element_type=jnp.float32)


def halves(value):
    high = value.astype(jnp.bfloat16)
    low = (value - high.astype(jnp.float32)).astype(jnp.bfloat16)
    return high, low


def gather_kernel(
    reps, feats, rank, rows, cols, total_feat,
    basis_hbm, stream_hbm, gram_ref, m_ref,
    w_ref, x_ref, whl_ref, sums_refs, recv_refs, av_ref,
    pay_ref, half_recv, half_sum, z_recv, full_ref,
    g_ref, g_core, g_sum, g_recv,
    load_sem, ring_send, ring_recv, core_send, core_recv, z_send, z_recv_sem,
    gz_send, gz_recv, hello_sem,
):
    bits = reps.bit_length() - 1
    chunk = LANE * reps
    chunks = cols // chunk
    zs = feats // 2
    me = lax.axis_index("rep")
    feat = lax.axis_index("feat")
    core = feat % 2
    zpos = feat // 2
    eta = learn_rate / rows
    scale = jnp.sqrt(jnp.float32(total_feat))

    loads = []
    for c in range(chunks):
        cut = slice(c * chunk, (c + 1) * chunk)
        loads.append(pltpu.make_async_copy(basis_hbm.at[:, cut], w_ref.at[:, cut], load_sem.at[c]))
        loads[c].start()
    load_x = pltpu.make_async_copy(stream_hbm, x_ref, load_sem.at[chunks])
    load_x.start()

    def rep_peer(b):
        bit = (me // (1 << b)) % 2
        return me + (1 - 2 * bit) * (1 << b), bit

    rep_ids = [(rep_peer(b)[0], feat) for b in range(bits)]
    core_id = (me, feat + 1 - 2 * core)
    z_ids = [(me, ((zpos + d) % zs) * 2 + core) for d in range(1, zs)]

    beside = (zpos > 0).astype(jnp.int32) + (zpos < zs - 1).astype(jnp.int32)

    def tell_beside(sem):
        for ahead, there in ((-1, zpos > 0), (1, zpos < zs - 1)):

            @pl.when(there)
            def _():
                pl.semaphore_signal(
                    sem, inc=1, device_id=(me, feat + 2 * ahead), device_id_type=MESH
                )

    barrier = pltpu.get_barrier_semaphore()
    for peer in rep_ids + [core_id]:
        pl.semaphore_signal(barrier, inc=1, device_id=peer, device_id_type=MESH)
    tell_beside(barrier)
    pl.semaphore_wait(barrier, bits + 1 + beside)

    def remote(src, dst, send_sem, recv_sem, peer):
        copy = pltpu.make_async_remote_copy(
            src_ref=src, dst_ref=dst, send_sem=send_sem, recv_sem=recv_sem,
            device_id=peer, device_id_type=MESH,
        )
        copy.start()
        return copy

    started = []

    def at(off, width):
        return pl.ds(pl.multiple_of(off, LANE), width)

    def order(c):
        return [(c + i) % bits for i in range(bits)]

    keeps = []
    for c in range(chunks):
        off = c * chunk
        rec = []
        for i, b in enumerate(order(c)):
            width = chunk >> (i + 1)
            bit = rep_peer(b)[1]
            off = off + bit * width
            rec.append(off)
        keeps.append(rec)

    ring = {}

    def send_scatter(c, i):
        b = order(c)[i]
        width = chunk >> (i + 1)
        bit = rep_peer(b)[1]
        other = (1 - bit) * width
        if i == 0:
            src = w_ref.at[:, at(c * chunk + other, width)]
        else:
            src = sums_refs[i - 1].at[:, at(c * 2 * width + other, width)]
        dst = recv_refs[i].at[:, c * width:(c + 1) * width]
        ring[c, i] = remote(src, dst, ring_send.at[i, c], ring_recv.at[i, c], rep_ids[b])

    def take_scatter(c, i):
        b = order(c)[i]
        width = chunk >> (i + 1)
        bit = rep_peer(b)[1]
        ring[c, i].wait_recv()
        if i == 0:
            own = w_ref[:, at(c * chunk + bit * width, width)]
        else:
            own = sums_refs[i - 1][:, at(c * 2 * width + bit * width, width)]
        total = own + recv_refs[i][:, c * width:(c + 1) * width]
        if i == bits - 1:
            av_ref[:, at(keeps[c][i], width)] = total / reps
        else:
            sums_refs[i][:, c * width:(c + 1) * width] = total

    def send_gather(c, i):
        s = bits - 1 - i
        b = order(c)[s]
        width = chunk >> (s + 1)
        piece = av_ref.at[:, at(keeps[c][s], width)]
        k = bits + i
        ring[c, k] = remote(piece, piece, ring_send.at[k, c], ring_recv.at[k, c], rep_ids[b])

    for c in range(chunks):
        loads[c].wait()
        send_scatter(c, 0)
    rounds = zs - 2
    if rounds > 0:
        tell_beside(hello_sem.at[0])

    def step(c, i):
        if i < bits:
            take_scatter(c, i)
        else:
            ring[c, i].wait_recv()
        if i + 1 < bits:
            send_scatter(c, i + 1)
        elif i + 1 < 2 * bits:
            send_gather(c, i + 1 - bits)

    pending = [(c, i) for i in range(2 * bits - 1) for c in range(chunks)]
    place = [0]

    def advance(count):
        for _ in range(count):
            if place[0] < len(pending):
                step(*pending[place[0]])
                place[0] += 1

    high, low = halves(w_ref[...])
    whl_ref[0:rank, :] = high
    whl_ref[rank:2 * rank, :] = low
    load_x.wait()
    x_all = x_ref[...]
    wx = fast_dot(whl_ref[...], x_all, NT)
    wx = wx[0:rank] + wx[rank:2 * rank]
    pay_ref[0:rank, :] = wx[:, 0:rows]
    pay_ref[rank:2 * rank, :] = wx[:, rows:2 * rows]
    pay_ref[2 * rank:2 * rank + rows, :] = fast_dot(x_ref[0:rows, :], x_ref[rows:2 * rows, :], NT)

    half = rank + rows // 2
    give = pl.ds(pl.multiple_of((1 - core) * half, 8), half)
    keep = pl.ds(pl.multiple_of(core * half, 8), half)
    core_copy = remote(pay_ref.at[give, :], half_recv, core_send.at[0], core_recv.at[0], core_id)
    advance(PLAN[0])
    core_copy.wait_recv()
    half_sum[...] = pay_ref[keep, :] + half_recv[...]
    for k in range(rounds):
        pl.semaphore_wait(hello_sem.at[k], beside)
        if k + 1 < rounds:
            tell_beside(hello_sem.at[k + 1])
    z_copies = [
        remote(half_sum, z_recv.at[d], z_send.at[d], z_recv_sem.at[d], z_ids[d])
        for d in range(zs - 1)
    ]
    started.append(core_copy)
    started.extend(z_copies)
    advance(PLAN[1])
    total = half_sum[...]
    for d in range(zs - 1):
        z_copies[d].wait_recv()
        total = total + z_recv[d]
    full_ref[keep, :] = total
    share = remote(full_ref.at[keep, :], full_ref.at[keep, :], core_send.at[1], core_recv.at[1], core_id)
    started.append(share)
    advance(PLAN[2])
    share.wait_recv()

    first = full_ref[0:rank, :]
    second = full_ref[rank:2 * rank, :]
    cross = full_ref[2 * rank:2 * rank + rows, :]
    proj0 = first / scale
    cov0 = exact_dot(proj0, proj0, NT)
    drive1 = exact_dot(proj0, cross, NN)
    proj1 = (second + eta * (drive1 - exact_dot(cov0, second, NN))) / scale
    cov1 = exact_dot(proj1, proj1, NT)
    advance(PLAN[3])
    k_w = eta * (eta * exact_dot(cov1, cov0, NN) - cov0 - cov1)
    k_x0 = eta * (proj0 - eta * exact_dot(cov1, proj0, NN))
    k_x1 = eta * proj1
    kwh, kwl = halves(k_w)
    kx = jnp.concatenate([k_x0, k_x1], axis=1)
    kxh, kxl = halves(kx)
    kx2 = jnp.concatenate([kxh, kxl], axis=0)
    kw2 = jnp.concatenate([kwh, kwl], axis=0)

    def unmixed(c):
        cut = slice(c * chunk, (c + 1) * chunk)
        part = fast_dot(kx2, x_ref[:, cut], NN) + fast_dot(kw2, whl_ref[0:rank, cut], NN)
        part = part[0:rank] + part[rank:2 * rank] + fast_dot(kwh, whl_ref[rank:2 * rank, cut], NN)
        m_ref[:, cut] = part

    for c in range(chunks):
        unmixed(c)
        advance(1)
    advance(len(pending))

    acc = [jnp.zeros((2 * rank, rank), jnp.float32)]

    def mix(off, width):
        cut = at(off, width)
        value = m_ref[:, cut] + av_ref[:, cut]
        m_ref[:, cut] = value
        mh, ml = halves(value)
        acc[0] = acc[0] + fast_dot(jnp.concatenate([mh, ml], axis=0), mh, NT)

    wide = chunk // 2
    for c in range(chunks):
        mix(keeps[c][0], wide)
    for c in range(chunks):
        ring[c, 2 * bits - 1].wait_recv()
        mix(2 * c * chunk + wide - keeps[c][0], wide)
    acc = acc[0]
    low_part = acc[rank:2 * rank]
    gram = (acc[0:rank] + (low_part + low_part.T)) / total_feat
    hr = rank // 2
    g_ref[...] = jnp.concatenate([gram[0:hr], gram[hr:rank]], axis=1)
    gc = remote(g_ref, g_core, core_send.at[2], core_recv.at[2], core_id)
    gc.wait_recv()
    g_sum[...] = g_ref[...] + g_core[...]
    g_copies = [
        remote(g_sum, g_recv.at[d], gz_send.at[d], gz_recv.at[d], z_ids[d]) for d in range(zs - 1)
    ]
    total = g_sum[...]
    for d in range(zs - 1):
        g_copies[d].wait_recv()
        total = total + g_recv[d]
    gram_ref[...] = total
    for copy in started + [gc] + g_copies + list(ring.values()):
        copy.wait_send()


def solve_kernel(rank, cols, gram_ref, m_ref, out_hbm, o_ref, out_sem):
    hr = rank // 2
    both = gram_ref[...]
    gram = jnp.concatenate([both[:, 0:rank], both[:, rank:2 * rank]], axis=0)
    eye = jnp.where(
        lax.broadcasted_iota(jnp.int32, (rank, rank), 0)
        == lax.broadcasted_iota(jnp.int32, (rank, rank), 1), 1.0, 0.0
    ).astype(jnp.float32)
    table = jnp.concatenate([gram, eye], axis=1)
    sub = 8
    blocks = [table[i * sub:(i + 1) * sub, :] for i in range(rank // sub)]
    ids = lax.broadcasted_iota(jnp.int32, (sub, 2 * rank), 0)
    pieces = 4
    width = cols // pieces
    outs = []

    def finish(lo, hi):
        part = jnp.concatenate(blocks[lo // sub:hi // sub], axis=0)
        diag = jnp.sum(part[:, 0:rank] * eye[lo:hi], axis=1, keepdims=True)
        th, tl = halves(part[:, rank:rank + hi] * lax.rsqrt(diag))
        left = jnp.concatenate([th, th, tl], axis=1)
        for p in range(pieces):
            cut = slice(p * width, (p + 1) * width)
            mh, ml = halves(m_ref[0:hi, cut])
            o_ref[lo:hi, cut] = fast_dot(left, jnp.concatenate([mh, ml, mh], axis=0), NN)
            copy = pltpu.make_async_copy(
                o_ref.at[lo:hi, cut], out_hbm.at[lo:hi, cut], out_sem.at[len(outs)]
            )
            copy.start()
            outs.append(copy)

    for j in range(0, rank, 4):
        if j == hr:
            finish(0, hr)
        b, r = divmod(j, sub)
        todo = range(b if r == 0 else b + 1, rank // sub)
        lanes = [jnp.broadcast_to(blocks[b][:, j + k:j + k + 1], (sub, 2 * rank)) for k in range(4)]
        cols4 = {
            i: [jnp.broadcast_to(blocks[i][:, j + k:j + k + 1], (sub, 2 * rank)) for k in range(4)]
            for i in todo if i != b
        }
        cols4[b] = lanes
        rows4 = [blocks[b][r + k:r + k + 1, :] for k in range(4)]
        d = [[lanes[l][r + k:r + k + 1, :] for l in range(4)] for k in range(4)]
        idet = 1.0 / (d[0][0] * d[1][1] - d[0][1] * d[1][0])
        i00, i01, i11 = d[1][1] * idet, -d[0][1] * idet, d[0][0] * idet
        y0 = i00 * rows4[0] + i01 * rows4[1]
        y1 = i01 * rows4[0] + i11 * rows4[1]
        y02, y12 = i00 * d[0][2] + i01 * d[1][2], i01 * d[0][2] + i11 * d[1][2]
        y03, y13 = i00 * d[0][3] + i01 * d[1][3], i01 * d[0][3] + i11 * d[1][3]
        e22 = d[2][2] - (d[2][0] * y02 + d[2][1] * y12)
        e23 = d[2][3] - (d[2][0] * y03 + d[2][1] * y13)
        e33 = d[3][3] - (d[3][0] * y03 + d[3][1] * y13)
        row2 = rows4[2] - (d[2][0] * y0 + d[2][1] * y1)
        row3 = rows4[3] - (d[3][0] * y0 + d[3][1] * y1)
        jdet = 1.0 / (e22 * e33 - e23 * e23)
        j00, j01, j11 = e33 * jdet, -e23 * jdet, e22 * jdet
        z0 = j00 * row2 + j01 * row3
        z1 = j01 * row2 + j11 * row3
        for i in todo:
            c = cols4[i]
            c2 = c[2] - (c[0] * y02 + c[1] * y12)
            c3 = c[3] - (c[0] * y03 + c[1] * y13)
            update = (c[0] * y0 + c[1] * y1) + (c2 * z0 + c3 * z1)
            if i == b:
                update = jnp.where(ids > r + 3, update, 0.0)
            blocks[i] = blocks[i] - update
        done = [
            rows4[0], rows4[1] - (d[0][1] / d[0][0]) * rows4[0],
            row2, row3 - (e23 / e22) * row2,
        ]
        block = blocks[b]
        for k in range(4):
            block = jnp.where(ids == r + k, done[k], block)
        blocks[b] = block
    finish(hr, rank)
    for copy in outs:
        copy.wait()


def per_device(basis, stream):
    reps = lax.axis_size("rep")
    feats = lax.axis_size("feat")
    start = basis[0]
    steps, rows, cols = stream.shape[1:]
    batches = stream[0].reshape(steps * rows, cols)
    rank = start.shape[0]
    bits = reps.bit_length() - 1
    chunk = LANE * reps
    chunks = cols // chunk
    zs = feats // 2
    half = rank + rows // 2
    f32 = jnp.float32
    vm = pltpu.VMEM
    hr = rank // 2
    dma = pltpu.SemaphoreType.DMA
    gram, mixed = pl.pallas_call(
        functools.partial(gather_kernel, reps, feats, rank, rows, cols, cols * feats),
        out_shape=(
            pltpu.VMEM((hr, 2 * rank), f32),
            pltpu.VMEM((rank, cols), f32),
        ),
        in_specs=[pl.BlockSpec(memory_space=pl.ANY)] * 2,
        out_specs=(pl.BlockSpec(memory_space=pltpu.VMEM), pl.BlockSpec(memory_space=pltpu.VMEM)),
        scratch_shapes=[
            vm((rank, cols), f32),
            vm((steps * rows, cols), jnp.bfloat16),
            vm((2 * rank, cols), jnp.bfloat16),
            [vm((rank, cols >> (i + 1)), f32) for i in range(bits)],
            [vm((rank, cols >> (i + 1)), f32) for i in range(bits)],
            vm((rank, cols), f32),
            vm((2 * half, rows), f32),
            vm((half, rows), f32),
            vm((half, rows), f32),
            vm((zs - 1, half, rows), f32),
            vm((2 * half, rows), f32),
            vm((hr, 2 * rank), f32),
            vm((hr, 2 * rank), f32),
            vm((hr, 2 * rank), f32),
            vm((zs - 1, hr, 2 * rank), f32),
            dma((chunks + 1,)),
            dma((2 * bits, chunks)),
            dma((2 * bits, chunks)),
            dma((3,)),
            dma((3,)),
            dma((zs - 1,)),
            dma((zs - 1,)),
            dma((zs - 1,)),
            dma((zs - 1,)),
            pltpu.SemaphoreType.REGULAR((max(zs - 2, 1),)),
        ],
        compiler_params=pltpu.CompilerParams(collective_id=0, has_side_effects=True),
    )(start, batches)
    result = pl.pallas_call(
        functools.partial(solve_kernel, rank, cols),
        out_shape=jax.ShapeDtypeStruct((rank, cols), f32),
        in_specs=[pl.BlockSpec(memory_space=pltpu.VMEM)] * 2,
        out_specs=pl.BlockSpec(memory_space=pl.ANY),
        scratch_shapes=[vm((rank, cols), f32), dma((8,))],
    )(
        pltpu.with_memory_space_constraint(gram, pltpu.VMEM),
        pltpu.with_memory_space_constraint(mixed, pltpu.VMEM),
    )
    return result[None]


def solution(mesh):
    placed = (P("rep", None, "feat"), P("rep", None, None, "feat"))
    return jax.shard_map(
        per_device, mesh=mesh, in_specs=placed, out_specs=P("rep", None, "feat"), check_vma=False
    )
```

profile of v0, /device:TPU:0, one launch (start us, length us, event | category | flops | bytes accessed | tf_op | source)
XLA Modules:
  0.0 32.2 jit_solution(2264390354014692614)
XLA Ops:
  0.0 28.8 %shard_map.28 = (f32[32,128]{1,0:T(8,128)S(1)}, f32[64,4096]{1,0:T(8,128)S(1)}) custom-call(f32[64,4096]{1,0:T(8,128)} %bitcast.4, bf16[256,4096]{1,0:T(8,128)(2,1)} %bitcast.3), custom_call_target="tpu_custom_call" | custom-call | tf_op jit(solution)/shard_map/pallas_call | solution.py:376
  28.9 3.4 %shard_map.29 = f32[64,4096]{1,0:T(8,128)} custom-call(f32[32,128]{1,0:T(8,128)S(1)} %get-tuple-element.7.gram_ref, f32[64,4096]{1,0:T(8,128)S(1)} %get-tuple-element.8.m_ref), custom_call_target="tpu_custom_call" | custom-call | tf_op jit(solution)/shard_map/pallas_call | solution.py:413
where the time goes:
time: 32.4 us; the launch traced here: 32.2 us
  Pallas kernels  32.2 us (99%)
    pallas_call x1, Pallas kernels, per_device(): pl.pallas_call(functools.partial(gather_kernel, reps, feats, rank, rows,...  28.8 us
    pallas_call x1, Pallas kernels, per_device(): pl.pallas_call(functools.partial(solve_kernel, rank, cols), out_shape=jax...  3.38 us

commit v1 on v0

--- a/solution.py
+++ b/solution.py
@@ -10,6 +10,10 @@
 learn_rate = 0.5
 LANE = 128
 PLAN = (2, 18, 3, 1)
+SUB = 8
+NB = 2
+PIECES = 4
+LATE = 2
 MESH = pl.DeviceIdType.MESH
 NN = (((1,), (0,)), ((), ()))
 NT = (((1,), (1,)), ((), ()))
@@ -33,12 +37,12 @@
 
 def gather_kernel(
     reps, feats, rank, rows, cols, total_feat,
-    basis_hbm, stream_hbm, gram_ref, m_ref,
-    w_ref, x_ref, whl_ref, sums_refs, recv_refs, av_ref,
+    basis_hbm, stream_hbm, gram_ref, mh_ref, ml_ref,
+    m_ref, w_ref, x_ref, whl_ref, sums_refs, recv_refs, av_ref,
     pay_ref, half_recv, half_sum, z_recv, full_ref,
-    g_ref, g_core, g_sum, g_recv,
+    g_ref, g_core, g_recv,
     load_sem, ring_send, ring_recv, core_send, core_recv, z_send, z_recv_sem,
-    gz_send, gz_recv, hello_sem,
+    gz_send, gz_recv, gx_send, gx_recv, hello_sem,
 ):
     bits = reps.bit_length() - 1
     chunk = LANE * reps
@@ -242,117 +246,172 @@
         advance(1)
     advance(len(pending))
 
-    acc = [jnp.zeros((2 * rank, rank), jnp.float32)]
-
-    def mix(off, width):
+    slim = [jnp.zeros((2 * rank, rank), jnp.float32)]
+    full = [jnp.zeros((rank, 2 * rank), jnp.float32)]
+
+    def mix(off, width, late):
         cut = at(off, width)
-        value = m_ref[:, cut] + av_ref[:, cut]
-        m_ref[:, cut] = value
-        mh, ml = halves(value)
-        acc[0] = acc[0] + fast_dot(jnp.concatenate([mh, ml], axis=0), mh, NT)
+        mh, ml = halves(m_ref[:, cut] + av_ref[:, cut])
+        mh_ref[:, cut] = mh
+        ml_ref[:, cut] = ml
+        both = jnp.concatenate([mh, ml], axis=0)
+        if late:
+            part = fast_dot(both, jnp.concatenate([mh, mh], axis=0), NT)
+            part = part[0:rank] + part[rank:2 * rank]
+            full[0] = full[0] + (part + fast_dot(mh, jnp.concatenate([ml, ml], axis=0), NT))
+        else:
+            slim[0] = slim[0] + fast_dot(both, mh, NT)
 
     wide = chunk // 2
     for c in range(chunks):
-        mix(keeps[c][0], wide)
-    for c in range(chunks):
+        mix(keeps[c][0], wide, False)
+    for c in range(chunks):
+        if c == chunks - LATE:
+            low_part = slim[0][rank:2 * rank]
+            early = slim[0][0:rank] + (low_part + low_part.T)
+            full[0] = full[0] + jnp.concatenate([early, early], axis=1)
         ring[c, 2 * bits - 1].wait_recv()
-        mix(2 * c * chunk + wide - keeps[c][0], wide)
-    acc = acc[0]
-    low_part = acc[rank:2 * rank]
-    gram = (acc[0:rank] + (low_part + low_part.T)) / total_feat
+        mix(2 * c * chunk + wide - keeps[c][0], wide, c >= chunks - LATE)
     hr = rank // 2
-    g_ref[...] = jnp.concatenate([gram[0:hr], gram[hr:rank]], axis=1)
-    gc = remote(g_ref, g_core, core_send.at[2], core_recv.at[2], core_id)
+    gram = full[0] / total_feat
+    lane = lax.broadcasted_iota(jnp.int32, (hr, 2 * rank), 1)
+    g_ref[...] = jnp.where(lane < rank, gram[0:hr], gram[hr:rank])
+    upper = (2 * zpos) // zs
+    g_copies = []
+    for j in range(zs - 1):
+        far = upper * (j + (j >= zpos).astype(jnp.int32))
+        near = (1 - upper) * (zs - 1 - j - (zs - 1 - j <= zpos).astype(jnp.int32))
+        peer = far + near
+        slot = (peer - zpos + zs) % zs - 1
+        for k in range(2):
+            other = (core + k) % 2
+            g_copies.append(remote(
+                g_ref, g_recv.at[k, slot], gz_send.at[k, slot], gz_recv.at[k, slot],
+                (me, peer * 2 + other),
+            ))
+    gc = remote(g_ref, g_core, gx_send.at[0], gx_recv.at[0], core_id)
     gc.wait_recv()
-    g_sum[...] = g_ref[...] + g_core[...]
-    g_copies = [
-        remote(g_sum, g_recv.at[d], gz_send.at[d], gz_recv.at[d], z_ids[d]) for d in range(zs - 1)
-    ]
-    total = g_sum[...]
-    for d in range(zs - 1):
-        g_copies[d].wait_recv()
-        total = total + g_recv[d]
+    total = g_ref[...] + g_core[...]
+    for copy in g_copies:
+        copy.wait_recv()
+    for k in range(2):
+        for d in range(zs - 1):
+            total = total + g_recv[k, d]
     gram_ref[...] = total
     for copy in started + [gc] + g_copies + list(ring.values()):
         copy.wait_send()
 
 
-def solve_kernel(rank, cols, gram_ref, m_ref, out_hbm, o_ref, out_sem):
+def lanes(block, lane):
+    return jnp.broadcast_to(block[:, lane:lane + 1], block.shape)
+
+def row(block, r):
+    return jnp.broadcast_to(block[r:r + 1, :], block.shape)
+
+def panel(blocks, first, nb, col, ids):
+    w = SUB * nb
+    last = len(blocks)
+    own = [blocks[first + v] for v in range(nb)]
+    d = [[lanes(own[v], col + k) for v in range(nb)] for k in range(w)]
+    c = {i: [lanes(blocks[i], col + k) for k in range(w)] for i in range(first + nb, last)}
+    done = []
+    for p in range(0, w, 2):
+        v, s = divmod(p, SUB)
+        a00, a10, a11 = row(d[p][v], s), row(d[p][v], s + 1), row(d[p + 1][v], s + 1)
+        idet = 1.0 / (a00 * a11 - a10 * a10)
+        i00, i01, i11 = a11 * idet, -(a10 * idet), a00 * idet
+        at0, at1 = ids == s, ids == s + 1
+
+        def step(x):
+            t0, t1 = row(x[v], s), row(x[v], s + 1)
+            z0 = i00 * t0 + i01 * t1
+            z1 = i01 * t0 + i11 * t1
+            out = []
+            for u in range(nb):
+                new = x[u] - (d[p][u] * z0 + d[p + 1][u] * z1)
+                if u == v:
+                    new = jnp.where(at0, z0, jnp.where(at1, z1, new))
+                out.append(new)
+            return t0, t1, out
+
+        r0, r1, new_own = step(own)
+        ratio = a10 / a00
+        done.append(r0 * lax.rsqrt(a00))
+        done.append((r1 - ratio * r0) * lax.rsqrt(a11 - ratio * a10))
+        new_d = {k: step(d[k])[2] for k in range(p + 2, w)}
+        own = new_own
+        for k in new_d:
+            d[k] = new_d[k]
+    if c:
+        z = [row(own[p // SUB], p % SUB) for p in range(w)]
+        for i in c:
+            parts = [c[i][p] * z[p] for p in range(w)]
+            while len(parts) > 1:
+                parts = [parts[q] + parts[q + 1] for q in range(0, len(parts), 2)]
+            blocks[i] = blocks[i] - parts[0]
+    res = []
+    for v in range(nb):
+        out = done[v * SUB]
+        for s in range(1, SUB):
+            out = jnp.where(ids == s, done[v * SUB + s], out)
+        res.append(out)
+    return res
+
+def solve_kernel(rank, cols, gram_ref, mh_ref, ml_ref, out_hbm, ph_ref, pl_ref, o_ref, out_sem):
     hr = rank // 2
+    n = rank // SUB
+    half = n // 2
+    lane = lax.broadcasted_iota(jnp.int32, (SUB, 2 * rank), 1)
+    ids = lax.broadcasted_iota(jnp.int32, (SUB, 2 * rank), 0)
     both = gram_ref[...]
-    gram = jnp.concatenate([both[:, 0:rank], both[:, rank:2 * rank]], axis=0)
-    eye = jnp.where(
-        lax.broadcasted_iota(jnp.int32, (rank, rank), 0)
-        == lax.broadcasted_iota(jnp.int32, (rank, rank), 1), 1.0, 0.0
-    ).astype(jnp.float32)
-    table = jnp.concatenate([gram, eye], axis=1)
-    sub = 8
-    blocks = [table[i * sub:(i + 1) * sub, :] for i in range(rank // sub)]
-    ids = lax.broadcasted_iota(jnp.int32, (sub, 2 * rank), 0)
-    pieces = 4
-    width = cols // pieces
+    zero = jnp.zeros((SUB, rank), jnp.float32)
+    top = [both[i * SUB:(i + 1) * SUB, :] for i in range(half)]
+    low = [jnp.concatenate([t[:, rank:2 * rank], zero], axis=1) for t in top]
+    blocks = [
+        jnp.where(lane < rank, top[i], jnp.where(lane == rank + ids + i * SUB, 1.0, 0.0))
+        for i in range(half)
+    ] + low
+    width = cols // PIECES
     outs = []
 
-    def finish(lo, hi):
-        part = jnp.concatenate(blocks[lo // sub:hi // sub], axis=0)
-        diag = jnp.sum(part[:, 0:rank] * eye[lo:hi], axis=1, keepdims=True)
-        th, tl = halves(part[:, rank:rank + hi] * lax.rsqrt(diag))
-        left = jnp.concatenate([th, th, tl], axis=1)
-        for p in range(pieces):
-            cut = slice(p * width, (p + 1) * width)
-            mh, ml = halves(m_ref[0:hi, cut])
-            o_ref[lo:hi, cut] = fast_dot(left, jnp.concatenate([mh, ml, mh], axis=0), NN)
-            copy = pltpu.make_async_copy(
-                o_ref.at[lo:hi, cut], out_hbm.at[lo:hi, cut], out_sem.at[len(outs)]
-            )
-            copy.start()
-            outs.append(copy)
-
-    for j in range(0, rank, 4):
-        if j == hr:
-            finish(0, hr)
-        b, r = divmod(j, sub)
-        todo = range(b if r == 0 else b + 1, rank // sub)
-        lanes = [jnp.broadcast_to(blocks[b][:, j + k:j + k + 1], (sub, 2 * rank)) for k in range(4)]
-        cols4 = {
-            i: [jnp.broadcast_to(blocks[i][:, j + k:j + k + 1], (sub, 2 * rank)) for k in range(4)]
-            for i in todo if i != b
-        }
-        cols4[b] = lanes
-        rows4 = [blocks[b][r + k:r + k + 1, :] for k in range(4)]
-        d = [[lanes[l][r + k:r + k + 1, :] for l in range(4)] for k in range(4)]
-        idet = 1.0 / (d[0][0] * d[1][1] - d[0][1] * d[1][0])
-        i00, i01, i11 = d[1][1] * idet, -d[0][1] * idet, d[0][0] * idet
-        y0 = i00 * rows4[0] + i01 * rows4[1]
-        y1 = i01 * rows4[0] + i11 * rows4[1]
-        y02, y12 = i00 * d[0][2] + i01 * d[1][2], i01 * d[0][2] + i11 * d[1][2]
-        y03, y13 = i00 * d[0][3] + i01 * d[1][3], i01 * d[0][3] + i11 * d[1][3]
-        e22 = d[2][2] - (d[2][0] * y02 + d[2][1] * y12)
-        e23 = d[2][3] - (d[2][0] * y03 + d[2][1] * y13)
-        e33 = d[3][3] - (d[3][0] * y03 + d[3][1] * y13)
-        row2 = rows4[2] - (d[2][0] * y0 + d[2][1] * y1)
-        row3 = rows4[3] - (d[3][0] * y0 + d[3][1] * y1)
-        jdet = 1.0 / (e22 * e33 - e23 * e23)
-        j00, j01, j11 = e33 * jdet, -e23 * jdet, e22 * jdet
-        z0 = j00 * row2 + j01 * row3
-        z1 = j01 * row2 + j11 * row3
-        for i in todo:
-            c = cols4[i]
-            c2 = c[2] - (c[0] * y02 + c[1] * y12)
-            c3 = c[3] - (c[0] * y03 + c[1] * y13)
-            update = (c[0] * y0 + c[1] * y1) + (c2 * z0 + c3 * z1)
-            if i == b:
-                update = jnp.where(ids > r + 3, update, 0.0)
-            blocks[i] = blocks[i] - update
-        done = [
-            rows4[0], rows4[1] - (d[0][1] / d[0][0]) * rows4[0],
-            row2, row3 - (e23 / e22) * row2,
-        ]
-        block = blocks[b]
-        for k in range(4):
-            block = jnp.where(ids == r + k, done[k], block)
-        blocks[b] = block
-    finish(hr, rank)
+    def send(lo, p):
+        cut = slice(p * width, (p + 1) * width)
+        copy = pltpu.make_async_copy(
+            o_ref.at[lo:lo + hr, cut], out_hbm.at[lo:lo + hr, cut], out_sem.at[len(outs)]
+        )
+        copy.start()
+        outs.append(copy)
+
+    def eliminate(first):
+        scaled = []
+        for b in range(first, first + half, NB):
+            scaled += panel(blocks, b, NB, b * SUB, ids)
+        return scaled
+
+    scaled = eliminate(0)
+    left = jnp.concatenate(scaled + blocks[half:], axis=0)[:, rank:rank + hr]
+    th, tl = halves(left)
+    thl = jnp.concatenate([th, tl], axis=0)
+    for p in range(PIECES):
+        cut = slice(p * width, (p + 1) * width)
+        part = fast_dot(thl, mh_ref[0:hr, cut], NN)
+        part = part[0:rank] + part[rank:2 * rank] + fast_dot(th, ml_ref[0:hr, cut], NN)
+        o_ref[0:hr, cut] = part[0:hr]
+        send(0, p)
+        rest = part[hr:rank] + mh_ref[hr:rank, cut].astype(jnp.float32)
+        rest = rest + ml_ref[hr:rank, cut].astype(jnp.float32)
+        ph_ref[:, cut], pl_ref[:, cut] = halves(rest)
+    for i in range(half):
+        unit = jnp.where(lane == ids + i * SUB, 1.0, 0.0)
+        blocks[half + i] = jnp.where(lane < hr, unit, blocks[half + i])
+    left = jnp.concatenate(eliminate(half), axis=0)[:, 0:hr]
+    th, tl = halves(left)
+    thl = jnp.concatenate([th, tl], axis=0)
+    for p in range(PIECES):
+        cut = slice(p * width, (p + 1) * width)
+        part = fast_dot(thl, ph_ref[:, cut], NN)
+        o_ref[hr:rank, cut] = part[0:hr] + part[hr:rank] + fast_dot(th, pl_ref[:, cut], NN)
+        send(hr, p)
     for copy in outs:
         copy.wait()
 
@@ -373,15 +432,17 @@
     vm = pltpu.VMEM
     hr = rank // 2
     dma = pltpu.SemaphoreType.DMA
-    gram, mixed = pl.pallas_call(
+    gram, mh, ml = pl.pallas_call(
         functools.partial(gather_kernel, reps, feats, rank, rows, cols, cols * feats),
         out_shape=(
             pltpu.VMEM((hr, 2 * rank), f32),
-            pltpu.VMEM((rank, cols), f32),
+            pltpu.VMEM((rank, cols), jnp.bfloat16),
+            pltpu.VMEM((rank, cols), jnp.bfloat16),
         ),
         in_specs=[pl.BlockSpec(memory_space=pl.ANY)] * 2,
-        out_specs=(pl.BlockSpec(memory_space=pltpu.VMEM), pl.BlockSpec(memory_space=pltpu.VMEM)),
+        out_specs=(pl.BlockSpec(memory_space=pltpu.VMEM),) * 3,
         scratch_shapes=[
+            vm((rank, cols), f32),
             vm((rank, cols), f32),
             vm((steps * rows, cols), jnp.bfloat16),
             vm((2 * rank, cols), jnp.bfloat16),
@@ -395,17 +456,18 @@
             vm((2 * half, rows), f32),
             vm((hr, 2 * rank), f32),
             vm((hr, 2 * rank), f32),
-            vm((hr, 2 * rank), f32),
-            vm((zs - 1, hr, 2 * rank), f32),
+            vm((2, zs - 1, hr, 2 * rank), f32),
             dma((chunks + 1,)),
             dma((2 * bits, chunks)),
             dma((2 * bits, chunks)),
-            dma((3,)),
-            dma((3,)),
+            dma((2,)),
+            dma((2,)),
             dma((zs - 1,)),
             dma((zs - 1,)),
-            dma((zs - 1,)),
-            dma((zs - 1,)),
+            dma((2, zs - 1)),
+            dma((2, zs - 1)),
+            dma((1,)),
+            dma((1,)),
             pltpu.SemaphoreType.REGULAR((max(zs - 2, 1),)),
         ],
         compiler_params=pltpu.CompilerParams(collective_id=0, has_side_effects=True),
@@ -413,12 +475,18 @@
     result = pl.pallas_call(
         functools.partial(solve_kernel, rank, cols),
         out_shape=jax.ShapeDtypeStruct((rank, cols), f32),
-        in_specs=[pl.BlockSpec(memory_space=pltpu.VMEM)] * 2,
+        in_specs=[pl.BlockSpec(memory_space=pltpu.VMEM)] * 3,
         out_specs=pl.BlockSpec(memory_space=pl.ANY),
-        scratch_shapes=[vm((rank, cols), f32), dma((8,))],
+        scratch_shapes=[
+            vm((hr, cols), jnp.bfloat16),
+            vm((hr, cols), jnp.bfloat16),
+            vm((rank, cols), f32),
+            dma((2 * PIECES,)),
+        ],
     )(
         pltpu.with_memory_space_constraint(gram, pltpu.VMEM),
-        pltpu.with_memory_space_constraint(mixed, pltpu.VMEM),
+        pltpu.with_memory_space_constraint(mh, pltpu.VMEM),
+        pltpu.with_memory_space_constraint(ml, pltpu.VMEM),
     )
     return result[None]
 

time: 32.4 us -> 31.5 us (0.972)
  Pallas kernels: 32.2 us -> 31.4 us
    pallas_call x1, Pallas kernels: 3.38 us -> 2.64 us  [per_device(): pl.pallas_call(functools.partial(solve_kernel, rank, cols), out_shape=jax...]
where the time goes in v1:
time: 31.5 us; the launch traced here: 31.4 us
  Pallas kernels  31.4 us (100%)
    pallas_call x1, Pallas kernels, per_device(): pl.pallas_call(functools.partial(gather_kernel, reps, feats, rank, rows,...  28.7 us
    pallas_call x1, Pallas kernels, per_device(): pl.pallas_call(functools.partial(solve_kernel, rank, cols), out_shape=jax...  2.64 us

profile of v1, /device:TPU:0, one launch (start us, length us, event | category | flops | bytes accessed | tf_op | source)
XLA Modules:
  0.0 31.4 jit_solution(5590678622337044203)
XLA Ops:
  0.0 28.7 %shard_map.28 = (f32[32,128]{1,0:T(8,128)S(1)}, bf16[64,4096]{1,0:T(8,128)(2,1)S(1)}, bf16[64,4096]{1,0:T(8,128)(2,1)S(1)}) custom-call(f32[64,4096]{1,0:T(8,128)} %bitcast.4, bf16[256,4096]{1,0:T(8,128)(2,1)} %bitcast.3), custom_call_target="tpu_custom_call" | custom-call | tf_op jit(solution)/shard_map/pallas_call | solution.py:435
  28.7 2.6 %shard_map.29 = f32[64,4096]{1,0:T(8,128)} custom-call(f32[32,128]{1,0:T(8,128)S(1)} %get-tuple-element.8.gram_ref, bf16[64,4096]{1,0:T(8,128)(2,1)S(1)} %get-tuple-element.9.mh_ref, bf16[64,4096]{1,0:T(8,128)(2,1)S(1)} %get-tuple-element.10.ml_ref), custom_call_target="tpu_custom_call" | custom-call | tf_op jit(solution)/shard_map/pallas_call | solution.py:475

commit v2 on v1

--- a/solution.py
+++ b/solution.py
@@ -312,7 +312,8 @@
     w = SUB * nb
     last = len(blocks)
     own = [blocks[first + v] for v in range(nb)]
-    d = [[lanes(own[v], col + k) for v in range(nb)] for k in range(w)]
+    keep = ids < w
+    d = [[jnp.where(keep, lanes(own[v], col + k), 0.0) for v in range(nb)] for k in range(w)]
     c = {i: [lanes(blocks[i], col + k) for k in range(w)] for i in range(first + nb, last)}
     done = []
     for p in range(0, w, 2):
@@ -320,28 +321,23 @@
         a00, a10, a11 = row(d[p][v], s), row(d[p][v], s + 1), row(d[p + 1][v], s + 1)
         idet = 1.0 / (a00 * a11 - a10 * a10)
         i00, i01, i11 = a11 * idet, -(a10 * idet), a00 * idet
-        at0, at1 = ids == s, ids == s + 1
+        at0, pair = ids == s, (ids == s) | (ids == s + 1)
+        e0 = [d[p][u] * i00 + d[p + 1][u] * i01 for u in range(nb)]
+        e1 = [d[p][u] * i01 + d[p + 1][u] * i11 for u in range(nb)]
+        e0[v] = jnp.where(pair, jnp.where(at0, -i00, -i01), e0[v])
+        e1[v] = jnp.where(pair, jnp.where(at0, -i01, -i11), e1[v])
 
         def step(x):
             t0, t1 = row(x[v], s), row(x[v], s + 1)
-            z0 = i00 * t0 + i01 * t1
-            z1 = i01 * t0 + i11 * t1
-            out = []
-            for u in range(nb):
-                new = x[u] - (d[p][u] * z0 + d[p + 1][u] * z1)
-                if u == v:
-                    new = jnp.where(at0, z0, jnp.where(at1, z1, new))
-                out.append(new)
-            return t0, t1, out
-
-        r0, r1, new_own = step(own)
+            base = [jnp.where(pair, 0.0, x[u]) if u == v else x[u] for u in range(nb)]
+            return t0, t1, [base[u] - (e0[u] * t0 + e1[u] * t1) for u in range(nb)]
+
+        r0, r1, own = step(own)
         ratio = a10 / a00
         done.append(r0 * lax.rsqrt(a00))
         done.append((r1 - ratio * r0) * lax.rsqrt(a11 - ratio * a10))
-        new_d = {k: step(d[k])[2] for k in range(p + 2, w)}
-        own = new_own
-        for k in new_d:
-            d[k] = new_d[k]
+        for k in range(p + 2, w):
+            d[k] = step(d[k])[2]
     if c:
         z = [row(own[p // SUB], p % SUB) for p in range(w)]
         for i in c:
@@ -356,7 +352,6 @@
             out = jnp.where(ids == s, done[v * SUB + s], out)
         res.append(out)
     return res
-
 def solve_kernel(rank, cols, gram_ref, mh_ref, ml_ref, out_hbm, ph_ref, pl_ref, o_ref, out_sem):
     hr = rank // 2
     n = rank // SUB

time: 31.5 us -> 31.1 us (0.987)
  Pallas kernels: 31.4 us -> 31 us
    pallas_call x1, Pallas kernels: 2.64 us -> 2.24 us  [per_device(): pl.pallas_call(functools.partial(solve_kernel, rank, cols), out_shape=jax...]
where the time goes in v2:
time: 31.1 us; the launch traced here: 31 us
  Pallas kernels  31 us (100%)
    pallas_call x1, Pallas kernels, per_device(): pl.pallas_call(functools.partial(gather_kernel, reps, feats, rank, rows,...  28.7 us
    pallas_call x1, Pallas kernels, per_device(): pl.pallas_call(functools.partial(solve_kernel, rank, cols), out_shape=jax...  2.24 us

profile of v2, /device:TPU:0, one launch (start us, length us, event | category | flops | bytes accessed | tf_op | source)
XLA Modules:
  0.0 31.0 jit_solution(2125920386556747307)
XLA Ops:
  0.0 28.7 %shard_map.28 = (f32[32,128]{1,0:T(8,128)S(1)}, bf16[64,4096]{1,0:T(8,128)(2,1)S(1)}, bf16[64,4096]{1,0:T(8,128)(2,1)S(1)}) custom-call(f32[64,4096]{1,0:T(8,128)} %bitcast.4, bf16[256,4096]{1,0:T(8,128)(2,1)} %bitcast.3), custom_call_target="tpu_custom_call" | custom-call | tf_op jit(solution)/shard_map/pallas_call | solution.py:430
  28.7 2.2 %shard_map.29 = f32[64,4096]{1,0:T(8,128)} custom-call(f32[32,128]{1,0:T(8,128)S(1)} %get-tuple-element.8.gram_ref, bf16[64,4096]{1,0:T(8,128)(2,1)S(1)} %get-tuple-element.9.mh_ref, bf16[64,4096]{1,0:T(8,128)(2,1)S(1)} %get-tuple-element.10.ml_ref), custom_call_target="tpu_custom_call" | custom-call | tf_op jit(solution)/shard_map/pallas_call | solution.py:470

commit v3 on v2

--- a/solution.py
+++ b/solution.py
@@ -40,9 +40,9 @@
     basis_hbm, stream_hbm, gram_ref, mh_ref, ml_ref,
     m_ref, w_ref, x_ref, whl_ref, sums_refs, recv_refs, av_ref,
     pay_ref, half_recv, half_sum, z_recv, full_ref,
-    g_ref, g_core, g_recv,
-    load_sem, ring_send, ring_recv, core_send, core_recv, z_send, z_recv_sem,
-    gz_send, gz_recv, gx_send, gx_recv, hello_sem,
+    g_ref, g_recv,
+    load_w, load_x_sem, ring_send, ring_recv, core_send, core_recv, z_send, z_recv_sem,
+    g_send, g_recv_sem, hello_sem,
 ):
     bits = reps.bit_length() - 1
     chunk = LANE * reps
@@ -55,14 +55,6 @@
     eta = learn_rate / rows
     scale = jnp.sqrt(jnp.float32(total_feat))
 
-    loads = []
-    for c in range(chunks):
-        cut = slice(c * chunk, (c + 1) * chunk)
-        loads.append(pltpu.make_async_copy(basis_hbm.at[:, cut], w_ref.at[:, cut], load_sem.at[c]))
-        loads[c].start()
-    load_x = pltpu.make_async_copy(stream_hbm, x_ref, load_sem.at[chunks])
-    load_x.start()
-
     def rep_peer(b):
         bit = (me // (1 << b)) % 2
         return me + (1 - 2 * bit) * (1 << b), bit
@@ -86,17 +78,22 @@
     for peer in rep_ids + [core_id]:
         pl.semaphore_signal(barrier, inc=1, device_id=peer, device_id_type=MESH)
     tell_beside(barrier)
+    load_basis = pltpu.make_async_copy(basis_hbm, w_ref, load_w)
+    load_basis.start()
+    load_x = pltpu.make_async_copy(stream_hbm, x_ref, load_x_sem)
+    load_x.start()
     pl.semaphore_wait(barrier, bits + 1 + beside)
 
-    def remote(src, dst, send_sem, recv_sem, peer):
-        copy = pltpu.make_async_remote_copy(
+    def link(src, dst, send_sem, recv_sem, peer):
+        return pltpu.make_async_remote_copy(
             src_ref=src, dst_ref=dst, send_sem=send_sem, recv_sem=recv_sem,
             device_id=peer, device_id_type=MESH,
         )
+
+    def remote(*args):
+        copy = link(*args)
         copy.start()
         return copy
-
-    started = []
 
     def at(off, width):
         return pl.ds(pl.multiple_of(off, LANE), width)
@@ -127,7 +124,7 @@
         else:
             src = sums_refs[i - 1].at[:, at(c * 2 * width + other, width)]
         dst = recv_refs[i].at[:, c * width:(c + 1) * width]
-        ring[c, i] = remote(src, dst, ring_send.at[i, c], ring_recv.at[i, c], rep_ids[b])
+        ring[c, i] = remote(src, dst, ring_send.at[0], ring_recv.at[i, c], rep_ids[b])
 
     def take_scatter(c, i):
         b = order(c)[i]
@@ -150,10 +147,10 @@
         width = chunk >> (s + 1)
         piece = av_ref.at[:, at(keeps[c][s], width)]
         k = bits + i
-        ring[c, k] = remote(piece, piece, ring_send.at[k, c], ring_recv.at[k, c], rep_ids[b])
-
+        ring[c, k] = remote(piece, piece, ring_send.at[1], ring_recv.at[k, c], rep_ids[b])
+
+    load_basis.wait()
     for c in range(chunks):
-        loads[c].wait()
         send_scatter(c, 0)
     rounds = zs - 2
     if rounds > 0:
@@ -192,7 +189,7 @@
     half = rank + rows // 2
     give = pl.ds(pl.multiple_of((1 - core) * half, 8), half)
     keep = pl.ds(pl.multiple_of(core * half, 8), half)
-    core_copy = remote(pay_ref.at[give, :], half_recv, core_send.at[0], core_recv.at[0], core_id)
+    core_copy = remote(pay_ref.at[give, :], half_recv, core_send, core_recv.at[0], core_id)
     advance(PLAN[0])
     core_copy.wait_recv()
     half_sum[...] = pay_ref[keep, :] + half_recv[...]
@@ -200,20 +197,16 @@
         pl.semaphore_wait(hello_sem.at[k], beside)
         if k + 1 < rounds:
             tell_beside(hello_sem.at[k + 1])
-    z_copies = [
-        remote(half_sum, z_recv.at[d], z_send.at[d], z_recv_sem.at[d], z_ids[d])
-        for d in range(zs - 1)
-    ]
-    started.append(core_copy)
-    started.extend(z_copies)
+    for d in range(zs - 1):
+        remote(half_sum, z_recv.at[d], z_send, z_recv_sem, z_ids[d])
     advance(PLAN[1])
     total = half_sum[...]
+    z_all = link(z_recv, z_recv, z_send, z_recv_sem, core_id)
+    z_all.wait_recv()
     for d in range(zs - 1):
-        z_copies[d].wait_recv()
         total = total + z_recv[d]
     full_ref[keep, :] = total
-    share = remote(full_ref.at[keep, :], full_ref.at[keep, :], core_send.at[1], core_recv.at[1], core_id)
-    started.append(share)
+    share = remote(full_ref.at[keep, :], full_ref.at[keep, :], core_send, core_recv.at[1], core_id)
     advance(PLAN[2])
     share.wait_recv()
 
@@ -273,33 +266,33 @@
         ring[c, 2 * bits - 1].wait_recv()
         mix(2 * c * chunk + wide - keeps[c][0], wide, c >= chunks - LATE)
     hr = rank // 2
-    gram = full[0] / total_feat
+    gram = full[0] * (1.0 / total_feat)
     lane = lax.broadcasted_iota(jnp.int32, (hr, 2 * rank), 1)
     g_ref[...] = jnp.where(lane < rank, gram[0:hr], gram[hr:rank])
     upper = (2 * zpos) // zs
-    g_copies = []
     for j in range(zs - 1):
         far = upper * (j + (j >= zpos).astype(jnp.int32))
         near = (1 - upper) * (zs - 1 - j - (zs - 1 - j <= zpos).astype(jnp.int32))
         peer = far + near
         slot = (peer - zpos + zs) % zs - 1
         for k in range(2):
-            other = (core + k) % 2
-            g_copies.append(remote(
-                g_ref, g_recv.at[k, slot], gz_send.at[k, slot], gz_recv.at[k, slot],
-                (me, peer * 2 + other),
-            ))
-    gc = remote(g_ref, g_core, gx_send.at[0], gx_recv.at[0], core_id)
-    gc.wait_recv()
-    total = g_ref[...] + g_core[...]
-    for copy in g_copies:
-        copy.wait_recv()
-    for k in range(2):
-        for d in range(zs - 1):
-            total = total + g_recv[k, d]
+            remote(
+                g_ref, g_recv.at[2 * slot + k], g_send, g_recv_sem,
+                (me, peer * 2 + (core + k) % 2),
+            )
+    remote(g_ref, g_recv.at[2 * zs - 2], g_send, g_recv_sem, core_id)
+    sent = cols - cols // reps
+    g_all = link(g_recv, g_recv, g_send, g_recv_sem, core_id)
+    link(w_ref.at[:, 0:sent], w_ref.at[:, 0:sent], ring_send.at[0], core_recv.at[0], core_id).wait_send()
+    link(w_ref.at[:, 0:sent], w_ref.at[:, 0:sent], ring_send.at[1], core_recv.at[0], core_id).wait_send()
+    link(pay_ref, pay_ref, core_send, core_recv.at[0], core_id).wait_send()
+    z_all.wait_send()
+    g_all.wait_send()
+    g_all.wait_recv()
+    total = g_ref[...]
+    for d in range(2 * zs - 1):
+        total = total + g_recv[d]
     gram_ref[...] = total
-    for copy in started + [gc] + g_copies + list(ring.values()):
-        copy.wait_send()
 
 
 def lanes(block, lane):
@@ -367,15 +360,13 @@
         for i in range(half)
     ] + low
     width = cols // PIECES
-    outs = []
 
     def send(lo, p):
         cut = slice(p * width, (p + 1) * width)
         copy = pltpu.make_async_copy(
-            o_ref.at[lo:lo + hr, cut], out_hbm.at[lo:lo + hr, cut], out_sem.at[len(outs)]
+            o_ref.at[lo:lo + hr, cut], out_hbm.at[lo:lo + hr, cut], out_sem
         )
         copy.start()
-        outs.append(copy)
 
     def eliminate(first):
         scaled = []
@@ -397,18 +388,22 @@
         rest = rest + ml_ref[hr:rank, cut].astype(jnp.float32)
         ph_ref[:, cut], pl_ref[:, cut] = halves(rest)
     for i in range(half):
-        unit = jnp.where(lane == ids + i * SUB, 1.0, 0.0)
-        blocks[half + i] = jnp.where(lane < hr, unit, blocks[half + i])
-    left = jnp.concatenate(eliminate(half), axis=0)[:, 0:hr]
+        unit = jnp.where(lane % hr == ids + i * SUB, 1.0, 0.0)
+        pivots = (lane >= hr) & (lane < rank)
+        blocks[half + i] = jnp.where(pivots, blocks[half + i], unit)
+    left = jnp.concatenate(eliminate(half), axis=0)
+    wide_lane = lax.broadcasted_iota(jnp.int32, (hr, 2 * rank), 1)
+    left = jnp.where((wide_lane >= hr) & (wide_lane < rank), 0.0, left)
     th, tl = halves(left)
-    thl = jnp.concatenate([th, tl], axis=0)
+    low_lane = (wide_lane >= rank) & (wide_lane < rank + hr)
+    mixed = jnp.where(low_lane, tl.astype(jnp.float32), th.astype(jnp.float32))
+    mixed = mixed.astype(jnp.bfloat16)
     for p in range(PIECES):
         cut = slice(p * width, (p + 1) * width)
-        part = fast_dot(thl, ph_ref[:, cut], NN)
-        o_ref[hr:rank, cut] = part[0:hr] + part[hr:rank] + fast_dot(th, pl_ref[:, cut], NN)
+        ph, pl_ = ph_ref[:, cut], pl_ref[:, cut]
+        o_ref[hr:rank, cut] = fast_dot(mixed, jnp.concatenate([ph, pl_, ph, pl_], axis=0), NN)
         send(hr, p)
-    for copy in outs:
-        copy.wait()
+    pltpu.make_async_copy(o_ref, out_hbm, out_sem).wait()
 
 
 def per_device(basis, stream):
@@ -450,19 +445,17 @@
             vm((zs - 1, half, rows), f32),
             vm((2 * half, rows), f32),
             vm((hr, 2 * rank), f32),
-            vm((hr, 2 * rank), f32),
-            vm((2, zs - 1, hr, 2 * rank), f32),
-            dma((chunks + 1,)),
+            vm((2 * zs - 1, hr, 2 * rank), f32),
+            dma,
+            dma,
+            dma((2,)),
             dma((2 * bits, chunks)),
-            dma((2 * bits, chunks)),
+            dma,
             dma((2,)),
-            dma((2,)),
-            dma((zs - 1,)),
-            dma((zs - 1,)),
-            dma((2, zs - 1)),
-            dma((2, zs - 1)),
-            dma((1,)),
-            dma((1,)),
+            dma,
+            dma,
+            dma,
+            dma,
             pltpu.SemaphoreType.REGULAR((max(zs - 2, 1),)),
         ],
         compiler_params=pltpu.CompilerParams(collective_id=0, has_side_effects=True),
@@ -476,7 +469,7 @@
             vm((hr, cols), jnp.bfloat16),
             vm((hr, cols), jnp.bfloat16),
             vm((rank, cols), f32),
-            dma((2 * PIECES,)),
+            dma,
         ],
     )(
         pltpu.with_memory_space_constraint(gram, pltpu.VMEM),

time: 31.1 us -> 30.7 us (0.987)
  Pallas kernels: 31 us -> 30.5 us
    pallas_call x1, Pallas kernels: 28.7 us -> 28.3 us  [per_device(): pl.pallas_call(functools.partial(gather_kernel, reps, feats, rank, rows,...]
where the time goes in v3:
time: 30.7 us; the launch traced here: 30.5 us
  Pallas kernels  30.5 us (99%)
    pallas_call x1, Pallas kernels, per_device(): pl.pallas_call(functools.partial(gather_kernel, reps, feats, rank, rows,...  28.3 us
    pallas_call x1, Pallas kernels, per_device(): pl.pallas_call(functools.partial(solve_kernel, rank, cols), out_shape=jax...  2.16 us

profile of v3, /device:TPU:0, one launch (start us, length us, event | category | flops | bytes accessed | tf_op | source)
XLA Modules:
  0.0 30.5 jit_solution(2956593625743943506)
XLA Ops:
  0.0 28.3 %shard_map.28 = (f32[32,128]{1,0:T(8,128)S(1)}, bf16[64,4096]{1,0:T(8,128)(2,1)S(1)}, bf16[64,4096]{1,0:T(8,128)(2,1)S(1)}) custom-call(f32[64,4096]{1,0:T(8,128)} %bitcast.4, bf16[256,4096]{1,0:T(8,128)(2,1)} %bitcast.3), custom_call_target="tpu_custom_call" | custom-call | tf_op jit(solution)/shard_map/pallas_call | solution.py:425
  28.3 2.2 %shard_map.29 = f32[64,4096]{1,0:T(8,128)} custom-call(f32[32,128]{1,0:T(8,128)S(1)} %get-tuple-element.8.gram_ref, bf16[64,4096]{1,0:T(8,128)(2,1)S(1)} %get-tuple-element.9.mh_ref, bf16[64,4096]{1,0:T(8,128)(2,1)S(1)} %get-tuple-element.10.ml_ref), custom_call_target="tpu_custom_call" | custom-call | tf_op jit(solution)/shard_map/pallas_call | solution.py:463

commit v4 on v3

--- a/solution.py
+++ b/solution.py
@@ -147,7 +147,7 @@
         width = chunk >> (s + 1)
         piece = av_ref.at[:, at(keeps[c][s], width)]
         k = bits + i
-        ring[c, k] = remote(piece, piece, ring_send.at[1], ring_recv.at[k, c], rep_ids[b])
+        ring[c, k] = remote(piece, piece, ring_send.at[1], ring_recv.at[k - 1 if i else 0, c], rep_ids[b])
 
     load_basis.wait()
     for c in range(chunks):
@@ -449,7 +449,7 @@
             dma,
             dma,
             dma((2,)),
-            dma((2 * bits, chunks)),
+            dma((2 * bits - 1, chunks)),
             dma,
             dma((2,)),
             dma,

time: 30.7 us -> 30.6 us (level)
  no operation moved by 1% of the time
where the time goes in v4:
time: 30.6 us; the launch traced here: 30.4 us
  Pallas kernels  30.4 us (99%)
    pallas_call x1, Pallas kernels, per_device(): pl.pallas_call(functools.partial(gather_kernel, reps, feats, rank, rows,...  28.3 us
    pallas_call x1, Pallas kernels, per_device(): pl.pallas_call(functools.partial(solve_kernel, rank, cols), out_shape=jax...  2.16 us

profile of v4, /device:TPU:0, one launch (start us, length us, event | category | flops | bytes accessed | tf_op | source)
XLA Modules:
  0.0 30.4 jit_solution(17986398496450294057)
XLA Ops:
  0.0 28.3 %shard_map.28 = (f32[32,128]{1,0:T(8,128)S(1)}, bf16[64,4096]{1,0:T(8,128)(2,1)S(1)}, bf16[64,4096]{1,0:T(8,128)(2,1)S(1)}) custom-call(f32[64,4096]{1,0:T(8,128)} %bitcast.4, bf16[256,4096]{1,0:T(8,128)(2,1)} %bitcast.3), custom_call_target="tpu_custom_call" | custom-call | tf_op jit(solution)/shard_map/pallas_call | solution.py:425
  28.3 2.2 %shard_map.29 = f32[64,4096]{1,0:T(8,128)} custom-call(f32[32,128]{1,0:T(8,128)S(1)} %get-tuple-element.8.gram_ref, bf16[64,4096]{1,0:T(8,128)(2,1)S(1)} %get-tuple-element.9.mh_ref, bf16[64,4096]{1,0:T(8,128)(2,1)S(1)} %get-tuple-element.10.ml_ref), custom_call_target="tpu_custom_call" | custom-call | tf_op jit(solution)/shard_map/pallas_call | solution.py:463

commit v5 on v4

--- a/solution.py
+++ b/solution.py
@@ -41,7 +41,7 @@
     m_ref, w_ref, x_ref, whl_ref, sums_refs, recv_refs, av_ref,
     pay_ref, half_recv, half_sum, z_recv, full_ref,
     g_ref, g_recv,
-    load_w, load_x_sem, ring_send, ring_recv, core_send, core_recv, z_send, z_recv_sem,
+    load_f, load_w, load_x_sem, ring_send, ring_recv, more_recv, core_send, core_recv, z_send, z_recv_sem,
     g_send, g_recv_sem, hello_sem,
 ):
     bits = reps.bit_length() - 1
@@ -78,7 +78,10 @@
     for peer in rep_ids + [core_id]:
         pl.semaphore_signal(barrier, inc=1, device_id=peer, device_id_type=MESH)
     tell_beside(barrier)
-    load_basis = pltpu.make_async_copy(basis_hbm, w_ref, load_w)
+    front = chunk * (chunks // 4)
+    load_front = pltpu.make_async_copy(basis_hbm.at[:, 0:front], w_ref.at[:, 0:front], load_f)
+    load_front.start()
+    load_basis = pltpu.make_async_copy(basis_hbm.at[:, front:cols], w_ref.at[:, front:cols], load_w)
     load_basis.start()
     load_x = pltpu.make_async_copy(stream_hbm, x_ref, load_x_sem)
     load_x.start()
@@ -147,10 +150,18 @@
         width = chunk >> (s + 1)
         piece = av_ref.at[:, at(keeps[c][s], width)]
         k = bits + i
-        ring[c, k] = remote(piece, piece, ring_send.at[1], ring_recv.at[k - 1 if i else 0, c], rep_ids[b])
-
-    load_basis.wait()
+        if i == 0:
+            done = ring_recv.at[0, c]
+        elif bits == 2 and c > 0:
+            done = ring_recv.at[1, c - 1]
+        else:
+            done = more_recv.at[i - 1, c]
+        ring[c, k] = remote(piece, piece, ring_send.at[1], done, rep_ids[b])
+
+    load_front.wait()
     for c in range(chunks):
+        if c == chunks // 4:
+            load_basis.wait()
         send_scatter(c, 0)
     rounds = zs - 2
     if rounds > 0:
@@ -448,8 +459,10 @@
             vm((2 * zs - 1, hr, 2 * rank), f32),
             dma,
             dma,
+            dma,
             dma((2,)),
-            dma((2 * bits - 1, chunks)),
+            dma((bits, chunks)),
+            dma((1, 1)) if bits == 2 else dma((bits - 1, chunks)),
             dma,
             dma((2,)),
             dma,

time: 30.6 us -> 30.4 us (level)
  no operation moved by 1% of the time
where the time goes in v5:
time: 30.4 us; the launch traced here: 30.2 us
  Pallas kernels  30.2 us (99%)
    pallas_call x1, Pallas kernels, per_device(): pl.pallas_call(functools.partial(gather_kernel, reps, feats, rank, rows,...  28 us
    pallas_call x1, Pallas kernels, per_device(): pl.pallas_call(functools.partial(solve_kernel, rank, cols), out_shape=jax...  2.17 us

profile of v5, /device:TPU:0, one launch (start us, length us, event | category | flops | bytes accessed | tf_op | source)
XLA Modules:
  0.0 30.2 jit_solution(1690503102602480817)
XLA Ops:
  0.0 28.0 %shard_map.28 = (f32[32,128]{1,0:T(8,128)S(1)}, bf16[64,4096]{1,0:T(8,128)(2,1)S(1)}, bf16[64,4096]{1,0:T(8,128)(2,1)S(1)}) custom-call(f32[64,4096]{1,0:T(8,128)} %bitcast.4, bf16[256,4096]{1,0:T(8,128)(2,1)} %bitcast.3), custom_call_target="tpu_custom_call" | custom-call | tf_op jit(solution)/shard_map/pallas_call | solution.py:436
  28.1 2.2 %shard_map.29 = f32[64,4096]{1,0:T(8,128)} custom-call(f32[32,128]{1,0:T(8,128)S(1)} %get-tuple-element.8.gram_ref, bf16[64,4096]{1,0:T(8,128)(2,1)S(1)} %get-tuple-element.9.mh_ref, bf16[64,4096]{1,0:T(8,128)(2,1)S(1)} %get-tuple-element.10.ml_ref), custom_call_target="tpu_custom_call" | custom-call | tf_op jit(solution)/shard_map/pallas_call | solution.py:476
